TPU v7x, 32 devices: a whole 2x2x4 slice. The times are simulated.
32 devices in a mesh: grp: 2 (over y), gz: 4 (over z), gx: 2 (over x), row: 2 (over core).
Axes of the slice: x: 2, y: 2, z: 4, core: 2. Of those that a mesh axis runs over, the one named last changes fastest.
Arguments:
- volume: float32 [32, 512, 512], P(('grp', 'gz'), 'gx', 'row'), parts along dimension 0, may hold values from -6 to 6
- tile_table: bfloat16 [64, 128, 128], replicated, may hold values from -0.09375 to 0.09375
- tile_ids: int32 [4, 2, 2, 4, 32], P('gz', 'gx', 'row'), may hold values from 0 to 63
- block_ids: int32 [4, 2, 2, 4, 768], P('gz', 'gx', 'row'), may hold values from 0 to 2047
- live_slots: int32 [4, 2, 2, 4], P('gz', 'gx', 'row'), may hold values from 4 to 32, as said below
- measured: float32 [8, 512, 16], P(('grp', 'gz'), ('gx', 'row')), parts along dimension 0, may hold values from -12 to 12
- row_norm: float32 [4, 512, 16], P('gz', ('gx', 'row')), may hold values from 0.2 to 1
- col_norm: float32 [16, 512, 512], P('gz', 'gx', 'row'), may hold values from 0.5 to 2
Outputs:
- new_volume: float32 [32, 512, 512], P(('grp', 'gz'), 'gx', 'row'), parts along dimension 0
There are 2 independent parts, one for each index of `grp`. A program takes and returns all parts, laid end to end along the dimension named above; an argument that names none is the same for every part. Nothing has to cross between parts.
Inputs may be any that keep to these rules, and one draw needn't show every extreme that they name: `block_ids`: indices of voxel blocks of the piece itself. `live_slots`: 32 is reached by some angle of some piece in every draw.
All inputs are finite; a program needn't handle non-finite values.
Results may differ from a plain program's by a relative error of at most 0.004.
Values may be sent and summed in bfloat16 or wider, within the bound.
A program may use at most 64 MiB of HBM per device.

v0:
```python
import functools

import jax
import jax.numpy as jnp
from jax import lax
from jax.experimental import pallas as pl
from jax.experimental.pallas import tpu as pltpu
from jax.sharding import PartitionSpec as P

MESH = pl.DeviceIdType.MESH
F_UNROLL = 8
B_UNROLL = 4
ACCS = 4
OUT_PARTS = 4
VMEM = 67043328


def project_kernel(
    sizes,
    tid_hbm,
    live_hbm,
    blocks,
    vol,
    table,
    meas_hbm,
    norm_hbm,
    res,
    tid,
    live,
    meas,
    norm,
    blk,
    tbl,
    vox,
    xs,
    acc,
    padw,
    sendw,
    recvw,
    tgt,
    part,
    peer,
    rim_lo,
    rim_hi,
    local_sem,
    wsend,
    wrecv,
    psend,
    precv,
    rsend,
    rrecv,
):
    nz, nx, nr = sizes
    pieces = nx * nr
    gz, gx, row = lax.axis_index("gz"), lax.axis_index("gx"), lax.axis_index("row")
    me = gx * nr + row
    angles, slots = tid.shape
    per_slot = blocks.shape[1] // slots
    tile = table.shape[1]
    rows, width = vol.shape
    runs = width // tile
    own_angles, det_rows, cols = meas.shape
    window = sendw.shape[3]
    depth = window - 2
    block_cols = per_slot // window
    groups, _, rim, _ = res.shape

    by_run = vox.reshape(rows, runs, 1, tile)
    small = [
        pltpu.make_async_copy(meas_hbm, meas, local_sem.at[runs + 1]),
        pltpu.make_async_copy(norm_hbm, norm, local_sem.at[runs + 2]),
    ]
    copies = [
        pltpu.make_async_copy(
            vol.at[:, pl.ds(h * tile, tile)], by_run.at[:, h, 0], local_sem.at[h]
        )
        for h in range(runs)
    ]
    copies.append(pltpu.make_async_copy(table, tbl, local_sem.at[runs]))
    copies += index_copies(blocks, blk, local_sem, runs + 5)
    copies.append(pltpu.make_async_copy(tid_hbm, tid, local_sem.at[runs + 3]))
    copies.append(pltpu.make_async_copy(live_hbm, live, local_sem.at[runs + 4]))
    for copy in small + copies:
        copy.start()

    barrier = pltpu.get_barrier_semaphore()
    others = [
        (dz, dx, dr)
        for dz in range(nz)
        for dx in range(nx)
        for dr in range(nr)
        if (dz, dx, dr) != (0, 0, 0)
    ]

    def at(dz, dx, dr):
        return {
            "gz": lax.rem(gz + dz, nz),
            "gx": lax.rem(gx + dx, nx),
            "row": lax.rem(row + dr, nr),
        }

    rim_lo[...] = jnp.zeros_like(rim_lo)
    rim_hi[...] = jnp.zeros_like(rim_hi)
    for offset in others:
        pl.semaphore_signal(barrier, inc=1, device_id=at(*offset), device_id_type=MESH)

    acc[...] = jnp.zeros_like(acc)
    padw[...] = jnp.zeros_like(padw)
    for copy in small:
        copy.wait()
    for oa in range(own_angles):
        for j, ref in enumerate((meas, norm)):
            padw[j, 1 : det_rows + 1, :] = ref[oa]
        for s in range(nz):
            for j in range(2):
                sendw[s, oa, j] = padw[j, s * depth : s * depth + window, :]
    recvw[gz, me] = sendw[gz]

    for copy in copies:
        copy.wait()

    per_angle = slots // F_UNROLL
    steps = angles * per_angle

    def gather(step):
        first = step * (F_UNROLL * per_slot)
        for j in range(F_UNROLL):
            for r in range(per_slot):
                at_row = blk[first + (j * per_slot + r)]
                xs[r : r + 1, j * tile : (j + 1) * tile] = vox[at_row]

    def forward(step, carry):
        a, k0 = step // per_angle, (step % per_angle) * F_UNROLL
        x = xs[...].astype(jnp.bfloat16)
        t = live_tiles(tbl, tid, live, a, k0, F_UNROLL)
        d = lax.dot_general(x, t, (((1,), (1,)), ((), ())), preferred_element_type=jnp.float32)
        gather(jnp.minimum(step + 1, steps - 1))
        acc[a] += d
        return carry

    slab = [(dx, dr) for dx in range(nx) for dr in range(nr)]
    early = max(3 * angles // 4, 1)
    spans = [(0, early)] + ([(early, angles - early)] if early < angles else [])

    def peer_copy(phase, n):
        span = pl.ds(*spans[phase])
        return pltpu.make_async_remote_copy(
            src_ref=part.at[:, span],
            dst_ref=peer.at[n - 1, :, span],
            send_sem=psend.at[phase, n - 1],
            recv_sem=precv.at[phase, n - 1],
            device_id=at(0, *slab[n]),
            device_id_type=MESH,
        )

    def rim_copy(phase, up, n):
        span = pl.ds(*spans[phase])
        there = at(0, *slab[n])
        there["gz"] = jnp.minimum(gz + 1, nz - 1) if up else jnp.maximum(gz - 1, 0)
        return pltpu.make_async_remote_copy(
            src_ref=part.at[groups - 1 if up else 0, span],
            dst_ref=(rim_lo if up else rim_hi).at[n, span],
            send_sem=rsend.at[phase, int(up), n],
            recv_sem=rrecv.at[phase, int(up), n],
            device_id=there,
            device_id_type=MESH,
        )

    def send(phase):
        first, count = spans[phase]
        for g in range(groups):
            for a in range(first, first + count):
                part[g, a] = acc[a, g * rim : (g + 1) * rim, :].astype(part.dtype)
        for n in range(1, pieces):
            peer_copy(phase, n).start()

        @pl.when(gz < nz - 1)
        def _():
            for n in range(pieces):
                rim_copy(phase, True, n).start()

        @pl.when(gz > 0)
        def _():
            for n in range(pieces):
                rim_copy(phase, False, n).start()

    gather(jnp.int32(0))
    lax.fori_loop(0, early * per_angle, forward, 0)
    pl.semaphore_wait(barrier, len(others))
    windows = []
    for n, offset in enumerate(others):
        there = at(*offset)
        windows.append(
            pltpu.make_async_remote_copy(
                src_ref=sendw.at[there["gz"]],
                dst_ref=recvw.at[gz, me],
                send_sem=wsend.at[n],
                recv_sem=wrecv.at[n],
                device_id=there,
                device_id_type=MESH,
            )
        )
        windows[-1].start()
    send(0)
    if len(spans) > 1:
        lax.fori_loop(early * per_angle, steps, forward, 0)
        send(1)

    for copy in windows:
        copy.wait()
    per_block = tile // cols
    for z in range(nz):
        for oa in range(own_angles):
            for j in range(2):
                for b in range(block_cols):
                    cut = [recvw[z, b * per_block + i, oa, j] for i in range(per_block)]
                    value = cut[0] if per_block == 1 else jnp.concatenate(cut, axis=1)
                    tgt[j, z * own_angles + oa, pl.ds(b, window, stride=block_cols), :] = value

    for phase in range(len(spans)):
        for n in range(1, pieces):
            peer_copy(phase, n).wait()

    @pl.when(gz < nz - 1)
    def _():
        for phase in range(len(spans)):
            for n in range(pieces):
                rim_copy(phase, True, n).wait_send()
                rim_copy(phase, False, n).wait_recv()

    @pl.when(gz > 0)
    def _():
        for phase in range(len(spans)):
            for n in range(pieces):
                rim_copy(phase, False, n).wait_send()
                rim_copy(phase, True, n).wait_recv()

    for g in range(groups):
        for a in range(angles):
            total = acc[a, g * rim : (g + 1) * rim, :]
            for n in range(pieces - 1):
                total = total + peer[n, g, a].astype(jnp.float32)
            if g == 0:
                for n in range(pieces):
                    total = total + rim_lo[n, a].astype(jnp.float32)
            if g == groups - 1:
                for n in range(pieces):
                    total = total + rim_hi[n, a].astype(jnp.float32)
            rows_in = slice(g * rim, (g + 1) * rim)
            value = tgt[1, a, rows_in, :] * (tgt[0, a, rows_in, :] - total)
            res[g, a] = value.astype(res.dtype)


def index_copies(blocks, blk, sem, base):
    angles, length = blocks.shape
    return [
        pltpu.make_async_copy(blocks.at[a], blk.at[pl.ds(a * length, length)], sem.at[base + a])
        for a in range(angles)
    ]


def live_tiles(tbl, tid, live, a, k0, count):
    tiles = []
    for j in range(count):
        picked = tbl[tid[a, k0 + j]]
        tiles.append(jnp.where(k0 + j < live[a], picked, jnp.zeros_like(picked)))
    return jnp.concatenate(tiles, axis=1)


def back_kernel(
    tid_hbm, live_hbm, blocks, res_hbm, table, vol, norm, out, tid, live, res, blk, tbl, volv,
    normv, outv, rs, ss, todo, sem, out_sem, *accs
):
    angles, slots = tid.shape
    per_slot = blocks.shape[1] // slots
    tile = tbl.shape[1]
    rows, width = vol.shape
    runs = width // tile
    groups, _, rim, _ = res.shape
    small = [
        pltpu.make_async_copy(live_hbm, live, sem.at[3]),
        pltpu.make_async_copy(res_hbm, res, sem.at[4]),
    ]
    indices = [pltpu.make_async_copy(table, tbl, sem.at[2])]
    indices.append(pltpu.make_async_copy(tid_hbm, tid, sem.at[5]))
    indices += index_copies(blocks, blk, sem, 6)
    copies = [
        pltpu.make_async_copy(vol, volv, sem.at[0]),
        pltpu.make_async_copy(norm, normv, sem.at[1]),
    ]
    for copy in small + indices:
        copy.start()
    chunk = 64

    def clear(i, carry):
        for ref in accs:
            ref[pl.ds(pl.multiple_of(i * chunk, chunk), chunk), :] = jnp.zeros(
                (chunk, tile), jnp.float32
            )
        return carry

    lax.fori_loop(0, runs * rows // chunk, clear, 0)
    for copy in small:
        copy.wait()
    per_angle = slots // B_UNROLL
    count = jnp.int32(0)
    for a in range(angles):
        need = (live[a] + B_UNROLL - 1) // B_UNROLL

        def put(i, c, a=a):
            todo[c] = a * per_angle + i
            return c + 1

        count = lax.fori_loop(0, need, put, count)
        rs[a] = jnp.concatenate([res[g, a].astype(jnp.float32) for g in range(groups)], axis=0)

    for copy in indices:
        copy.wait()
    for copy in copies:
        copy.start()

    def spread(step):
        a, k0 = step // per_angle, (step % per_angle) * B_UNROLL
        t = live_tiles(tbl, tid, live, a, k0, B_UNROLL)
        return jnp.dot(rs[a].astype(jnp.bfloat16), t, preferred_element_type=jnp.float32)

    def back(i, carry):
        later = spread(todo[jnp.maximum(jnp.minimum(i + 1, count - 1), 0)])
        first = todo[i] * (B_UNROLL * per_slot)
        for j in range(B_UNROLL):
            for r in range(per_slot):
                at_row = blk[first + (j * per_slot + r)]
                accs[r % ACCS][pl.ds(at_row, 1), :] += ss[r : r + 1, j * tile : (j + 1) * tile]
        ss[...] = later
        return carry

    ss[...] = spread(todo[0])
    lax.fori_loop(0, count, back, 0)

    for copy in copies:
        copy.wait()
    size = rows // OUT_PARTS
    sub = 32
    outs = []
    for p in range(OUT_PARTS):

        def join(i, carry, p=p):
            first = pl.multiple_of(p * size + i * sub, sub)
            for h in range(runs):
                lanes = slice(h * tile, (h + 1) * tile)
                part = pl.ds(pl.multiple_of(first * runs, sub * runs), sub * runs)
                lane = pl.ds(h, sub, stride=runs)
                total = accs[0].at[part][lane, :]
                for ref in accs[1:]:
                    total = total + ref.at[part][lane, :]
                outv[pl.ds(first, sub), lanes] = (
                    volv[pl.ds(first, sub), lanes] + normv[pl.ds(first, sub), lanes] * total
                )
            return carry

        lax.fori_loop(0, size // sub, join, 0)
        part = pl.ds(p * size, size)
        outs.append(pltpu.make_async_copy(outv.at[part], out.at[part], out_sem.at[p]))
        outs[-1].start()
    for copy in outs:
        copy.wait()


def on_device(sizes, volume, tile_table, tile_ids, block_ids, live_slots, measured, row_norm, col_norm):
    nz, nx, nr = sizes
    pieces = nx * nr
    depth, column_width, half_width = volume.shape
    tile = tile_table.shape[1]
    angles, slots = tile_ids.shape[3], tile_ids.shape[4]
    window = depth + 2
    per_slot = block_ids.shape[4] // slots
    block_cols = per_slot // window
    rim = 2 * block_cols
    groups = window // 2
    runs = half_width // tile
    rows = depth * column_width
    measured = measured.transpose(0, 2, 1)
    row_norm = row_norm.transpose(0, 2, 1)
    own_angles, det_rows, cols = measured.shape
    vmem = pl.BlockSpec(memory_space=pltpu.VMEM)
    hbm = pl.BlockSpec(memory_space=pltpu.HBM)

    live = live_slots.reshape(angles)
    blocks = block_ids.reshape(angles, slots * per_slot)
    tid = tile_ids.reshape(angles, slots)
    index = pltpu.SMEM((angles * slots * per_slot,), jnp.int32)
    chosen = pltpu.SMEM((angles, slots), jnp.int32)
    counts = pltpu.SMEM((angles,), jnp.int32)
    vol = volume.reshape(rows, half_width)
    norm = col_norm.reshape(rows, half_width)
    n_others = nz * pieces - 1
    n_peers = max(pieces - 1, 1)
    dma = pltpu.SemaphoreType.DMA
    f32, bf16 = jnp.float32, jnp.bfloat16

    res = pl.pallas_call(
        functools.partial(project_kernel, sizes),
        out_shape=jax.ShapeDtypeStruct((groups, angles, rim, tile), bf16),
        in_specs=[hbm] * 7,
        out_specs=vmem,
        scratch_shapes=[
            chosen,
            counts,
            pltpu.VMEM(measured.shape, f32),
            pltpu.VMEM(measured.shape, f32),
            index,
            pltpu.VMEM(tile_table.shape, tile_table.dtype),
            pltpu.VMEM((rows * runs, 1, tile), f32),
            pltpu.VMEM((per_slot, F_UNROLL * tile), f32),
            pltpu.VMEM((angles, per_slot, tile), f32),
            pltpu.VMEM((2, det_rows + 2, cols), f32),
            pltpu.VMEM((nz, own_angles, 2, window, cols), f32),
            pltpu.VMEM((nz, pieces, own_angles, 2, window, cols), f32),
            pltpu.VMEM((2, angles, per_slot, tile), f32),
            pltpu.VMEM((groups, angles, rim, tile), bf16),
            pltpu.VMEM((n_peers, groups, angles, rim, tile), bf16),
            pltpu.VMEM((pieces, angles, rim, tile), bf16),
            pltpu.VMEM((pieces, angles, rim, tile), bf16),
            dma((runs + 5 + angles,)),
            dma((n_others,)),
            dma((n_others,)),
            dma((2, n_peers)),
            dma((2, n_peers)),
            dma((2, 2, pieces)),
            dma((2, 2, pieces)),
        ],
        compiler_params=pltpu.CompilerParams(
            collective_id=0, has_side_effects=True, vmem_limit_bytes=VMEM
        ),
        name="project",
    )(tid, live, blocks, vol, tile_table, measured, row_norm)

    out = pl.pallas_call(
        back_kernel,
        out_shape=jax.ShapeDtypeStruct((rows, half_width), f32),
        in_specs=[hbm] * 7,
        out_specs=hbm,
        scratch_shapes=[
            chosen,
            counts,
            pltpu.VMEM((groups, angles, rim, tile), bf16),
            index,
            pltpu.VMEM(tile_table.shape, tile_table.dtype),
            pltpu.VMEM((rows, half_width), f32),
            pltpu.VMEM((rows, half_width), f32),
            pltpu.VMEM((rows, half_width), f32),
            pltpu.VMEM((angles, per_slot, tile), f32),
            pltpu.VMEM((per_slot, B_UNROLL * tile), f32),
            pltpu.SMEM((angles * slots // B_UNROLL,), jnp.int32),
            dma((6 + angles,)),
            dma((OUT_PARTS,)),
        ]
        + [pltpu.VMEM((runs * rows, tile), f32)] * ACCS,
        compiler_params=pltpu.CompilerParams(vmem_limit_bytes=VMEM),
        name="spread_back",
    )(tid, live, blocks, res, tile_table, vol, norm)
    return out.reshape(volume.shape)


def solution(mesh):
    placed = (
        P(("grp", "gz"), "gx", "row"),
        P(),
        P("gz", "gx", "row", None, None),
        P("gz", "gx", "row", None, None),
        P("gz", "gx", "row", None),
        P(("grp", "gz"), ("gx", "row"), None),
        P("gz", ("gx", "row"), None),
        P("gz", "gx", "row"),
    )
    sizes = (mesh.shape["gz"], mesh.shape["gx"], mesh.shape["row"])
    return jax.shard_map(
        functools.partial(on_device, sizes),
        mesh=mesh,
        in_specs=placed,
        out_specs=P(("grp", "gz"), "gx", "row"),
        check_vma=False,
    )
```

profile of v0, /device:TPU:1, one launch (start us, length us, event | category | flops | bytes accessed | tf_op | source)
XLA Modules:
  0.0 21.4 jit_solution(9389779072475094649)
XLA Ops:
  0.0 14.2 %project.1.res_hbm = bf16[3,4,8,128]{3,2,1,0:T(8,128)(2,1)} custom-call(s32[4,32]{1,0:T(4,128)} %bitcast.15, s32[4]{0:T(128)} %bitcast.17, s32[4,768]{1,0:T(4,128)} %bitcast.11, f32[1024,256]{1,0:T(8,128)} %bitcast.8, bf16[64,128,128]{2,1,0:T(8,128)(2,1)} %table.3, f32[1,16,128]{2,1,0:T(8,128)} %bitcast.13, f32[1,16,128]{2,1,0:T(8,128)} %bitcast.14), custom_call_target="tpu_custom_call" | custom-call | tf_op jit(solution)/shard_map/project/pallas_call | solution.py:401
  14.2 7.2 %spread_back.1 = f32[1024,256]{1,0:T(8,128)} custom-call(s32[4,32]{1,0:T(4,128)} %bitcast.16, s32[4]{0:T(128)} %bitcast.18, s32[4,768]{1,0:T(4,128)} %bitcast.12, bf16[3,4,8,128]{3,2,1,0:T(8,128)(2,1)} %project.1.res_hbm, bf16[64,128,128]{2,1,0:T(8,128)(2,1)} %table.3, f32[1024,256]{1,0:T(8,128)} %bitcast.9, f32[1024,256]{1,0:T(8,128)} %bitcast.10), custom_call_target="tpu_custom_call" | custom-call | tf_op jit(solution)/shard_map/spread_back/pallas_call | solution.py:438
where the time goes:
time: 21.5 us; the launch traced here: 21.4 us
  Pallas kernels  21.4 us (100%)
    pallas_call x1, Pallas kernels, on_device(): pl.pallas_call(functools.partial(project_kernel, sizes), out_shape=jax.Sh...  14.2 us
    pallas_call x1, Pallas kernels, on_device(): pl.pallas_call(back_kernel, out_shape=jax.ShapeDtypeStruct((rows, half_wi...  7.22 us

commit v1 on v0

--- a/solution.py
+++ b/solution.py
@@ -10,7 +10,7 @@
 MESH = pl.DeviceIdType.MESH
 F_UNROLL = 8
 B_UNROLL = 4
-ACCS = 4
+ACCS = 8
 OUT_PARTS = 4
 VMEM = 67043328
 

time: 21.5 us -> 21.4 us (level)
  no operation moved by 1% of the time
where the time goes in v1:
time: 21.4 us; the launch traced here: 21.2 us
  Pallas kernels  21.2 us (99%)
    pallas_call x1, Pallas kernels, on_device(): pl.pallas_call(functools.partial(project_kernel, sizes), out_shape=jax.Sh...  14.2 us
    pallas_call x1, Pallas kernels, on_device(): pl.pallas_call(back_kernel, out_shape=jax.ShapeDtypeStruct((rows, half_wi...  7.09 us

profile of v1, /device:TPU:1, one launch (start us, length us, event | category | flops | bytes accessed | tf_op | source)
XLA Modules:
  0.0 21.2 jit_solution(7523206493759048193)
XLA Ops:
  0.0 14.2 %project.1.res_hbm = bf16[3,4,8,128]{3,2,1,0:T(8,128)(2,1)} custom-call(s32[4,32]{1,0:T(4,128)} %bitcast.15, s32[4]{0:T(128)} %bitcast.17, s32[4,768]{1,0:T(4,128)} %bitcast.11, f32[1024,256]{1,0:T(8,128)} %bitcast.8, bf16[64,128,128]{2,1,0:T(8,128)(2,1)} %table.3, f32[1,16,128]{2,1,0:T(8,128)} %bitcast.13, f32[1,16,128]{2,1,0:T(8,128)} %bitcast.14), custom_call_target="tpu_custom_call" | custom-call | tf_op jit(solution)/shard_map/project/pallas_call | solution.py:401
  14.2 7.1 %spread_back.1 = f32[1024,256]{1,0:T(8,128)} custom-call(s32[4,32]{1,0:T(4,128)} %bitcast.16, s32[4]{0:T(128)} %bitcast.18, s32[4,768]{1,0:T(4,128)} %bitcast.12, bf16[3,4,8,128]{3,2,1,0:T(8,128)(2,1)} %project.1.res_hbm, bf16[64,128,128]{2,1,0:T(8,128)(2,1)} %table.3, f32[1024,256]{1,0:T(8,128)} %bitcast.9, f32[1024,256]{1,0:T(8,128)} %bitcast.10), custom_call_target="tpu_custom_call" | custom-call | tf_op jit(solution)/shard_map/spread_back/pallas_call | solution.py:438
